TPU v7x, 256 devices: a whole 4x4x8 slice. The times are simulated.
256 devices in a mesh: ang: 64 (over z_lo, x, y, core), box: 4 (over z_hi).
Axes of the slice: x: 4, y: 4, z: 8 (z_hi: 4, z_lo: 2; z = z_hi * 2 + z_lo), core: 2. Of those that a mesh axis runs over, the one named last changes fastest.
Arguments:
- incoming: float32 [2, 32, 32, 32768], P(None, None, 'box', 'ang'), may hold values from -6 to 6
- own_field: bfloat16 [2, 32, 256, 8192], P(None, None, 'box', 'ang'), may hold values from -6 to 6
- phase_mid: float32 [256, 8192], P('box', 'ang'), may hold values from -3.140625 to 3.140625
- phase_leaf: float32 [2048, 2048], P(('ang', 'box')), may hold values from -3.140625 to 3.140625
- phase_low: float32 [16384, 512], P(('ang', 'box')), may hold values from -3.140625 to 3.140625
- weight_top: float32 [4, 32768], P(None, 'ang'), may hold values from -0.3 to 1
- weight_leaf: float32 [4, 8192], replicated, may hold values from -0.3 to 1
- weight_low: float32 [4, 2048], replicated, may hold values from -0.3 to 1
- offsets: int32 [4], replicated, may hold values from -2 to 2, as said below
- owner: int32 [4, 64], replicated, may hold values from 0 to 63, each once within a row
Outputs:
- lower_field: float32 [2, 32, 16384, 512], P(None, None, ('ang', 'box'))
Inputs may be any that keep to these rules, and one draw needn't show every extreme that they name: `offsets`: the first entry is -2 and the last is 2. `owner`: each row is a permutation of the ang indices.
All inputs are finite; a program needn't handle non-finite values.
Results may differ from a plain program's by a relative error of at most 0.0003.
Values sent between devices are 32-bit elements; how exact they have to be, the bound alone decides.
No kernel may reach another device: no remote copies, remote signals or barrier semaphores. Data moves between devices by JAX's collectives and lax.ppermute only.
A program may use at most 64 MiB of HBM per device.

v0:
```python
import jax
import jax.numpy as jnp
from jax import lax
from jax.sharding import PartitionSpec as P

STENCIL = 4
REACH = 2
RATIO = 4
CHILDREN = 8


def from_behind(value, axis, by):
    count = lax.axis_size(axis)
    return lax.ppermute(value, axis, [(i, (i + by) % count) for i in range(count)])


def grouped(fine, row):
    shape = fine.shape
    return (fine * row).reshape(shape[:-1] + (shape[-1] // RATIO, RATIO)).sum(axis=-1)


def spread(fine, weights, offsets):
    width = fine.shape[-1] // RATIO
    last = fine.ndim - 1
    total = jnp.zeros(fine.shape[:-1] + (width + 2 * REACH,), jnp.float32)
    for index in range(STENCIL):
        placed = lax.dynamic_update_slice_in_dim(
            jnp.zeros_like(total), grouped(fine, weights[index]), REACH + offsets[index], last
        )
        total = total + placed
    return total


def wrapped(fine, weights, offsets):
    total = jnp.zeros(fine.shape[:-1] + (fine.shape[-1] // RATIO,), jnp.float32)
    for index in range(STENCIL):
        total = total + jnp.roll(grouped(fine, weights[index]), offsets[index], axis=-1)
    return total


def rotate(field, angle):
    cosine = jnp.cos(angle)
    sine = jnp.sin(angle)
    return jnp.stack([field[0] * cosine - field[1] * sine, field[0] * sine + field[1] * cosine])


def body(
    incoming,
    own_field,
    phase_mid,
    phase_leaf,
    phase_low,
    weight_top,
    weight_leaf,
    weight_low,
    offsets,
    owner,
):
    total = spread(incoming, weight_top, offsets)
    from_lower = from_behind(total[..., -REACH:], "ang", 1)
    from_upper = from_behind(total[..., :REACH], "ang", -1)
    coarse_top = total[..., REACH:-REACH]
    coarse_top = coarse_top.at[..., :REACH].add(from_lower).at[..., -REACH:].add(from_upper)
    children = jnp.repeat(coarse_top, CHILDREN, axis=2)
    mid = rotate(children, phase_mid) + own_field.astype(jnp.float32)
    group = lax.axis_index("box")
    row = lax.dynamic_index_in_dim(owner, group, 0, keepdims=False)
    order = jnp.zeros_like(row).at[row].set(jnp.arange(row.shape[0], dtype=jnp.int32))
    sent = jnp.take(mid, order, axis=2)
    mine = lax.all_to_all(sent, "ang", split_axis=2, concat_axis=3, tiled=True)
    parent = wrapped(mine, weight_leaf, offsets)
    leaves = jnp.broadcast_to(parent, (2, parent.shape[1], CHILDREN, parent.shape[3]))
    leaf_field = rotate(leaves, phase_leaf)
    coarse_low = wrapped(leaf_field, weight_low, offsets)
    lows = jnp.repeat(coarse_low, CHILDREN, axis=2)
    return rotate(lows, phase_low)


def solution(mesh):
    placed = (
        P(None, None, "box", "ang"),
        P(None, None, "box", "ang"),
        P("box", "ang"),
        P(("ang", "box"), None),
        P(("ang", "box"), None),
        P(None, "ang"),
        P(),
        P(),
        P(),
        P(),
    )
    return jax.shard_map(
        body,
        mesh=mesh,
        in_specs=placed,
        out_specs=P(None, None, ("ang", "box"), None),
        check_vma=False,
    )
```

profile of v0, /device:TPU:1, one launch (start us, length us, event | category | flops | bytes accessed | tf_op | source)
XLA Modules:
  0.0 164.4 jit_solution(697796897214931741)
XLA Ops:
  0.0 1.5 fusion.30
  7.4 2.8 %broadcast_multiply_fusion = (f32[2,32,8,512]{3,2,1,0:T(8,128)S(1)}, f32[2,32,8,512]{3,2,1,0:T(8,128)S(1)}, f32[2,32,8,512]{3,2,1,0:T(8,128)}, f32[2,32,8,512]{3,2,1,0:T(8,128)S(1)}) fusion(f32[2,32,8,512]{3,2,1,0:T(8,128)} %param.18, f32[512]{0:T(512)S(1)} %bitcast.78, f32[512]{0:T(512)S(1)} %bitcast.79, f32[512]{0:T(512)S(1)} %bitcast.80, f32[512]{0:T(512)S(1)} %bitcast.81), kind=kLoop, calls=%fused_computation.65 | loop fusion | flops 1048576 | bytes 5251072 | tf_op jit(solution)/shard_map/mul | solution.py:19
  10.2 3.7 %copy.43 = f32[2,32,8,512]{1,2,3,0:T(8,128)} copy(f32[2,32,8,512]{3,2,1,0:T(8,128)} %get-tuple-element.57) | data formatting | bytes 2097152 | tf_op jit(solution)/shard_map/mul | solution.py:19
  14.0 2.8 %copy.44 = f32[2,32,8,512]{1,2,3,0:T(8,128)} copy(f32[2,32,8,512]{3,2,1,0:T(8,128)S(1)} %get-tuple-element.56) | data formatting | bytes 2097152 | tf_op jit(solution)/shard_map/mul | solution.py:19
  16.7 3.0 %reduce_sum.116 = f32[2,32,8,128]{1,2,3,0:T(8,128)S(1)} reduce(f32[2,32,8,128,4]{1,2,4,3,0:T(8,128)} %bitcast.66, f32[]{:T(128)} %constant.120.clone.1), dimensions={4}, to_apply=%region_1.0 | reduce | flops 196608 | bytes 1310724 | tf_op jit(solution)/shard_map/reduce_sum | solution.py:19
  19.7 4.0 %reduce_sum.117 = f32[2,32,8,128]{1,2,3,0:T(8,128)} reduce(f32[2,32,8,128,4]{1,2,4,3,0:T(8,128)} %bitcast.67, f32[]{:T(128)} %constant.120.clone.1), dimensions={4}, to_apply=%region_2.0 | reduce | flops 196608 | bytes 1310724 | tf_op jit(solution)/shard_map/reduce_sum | solution.py:19
  23.7 2.8 %copy.45 = f32[2,32,8,512]{1,2,3,0:T(8,128)} copy(f32[2,32,8,512]{3,2,1,0:T(8,128)S(1)} %get-tuple-element.58) | data formatting | bytes 2097152 | tf_op jit(solution)/shard_map/mul | solution.py:19
  26.5 4.0 %reduce_sum.118 = f32[2,32,8,128]{1,2,3,0:T(8,128)} reduce(f32[2,32,8,128,4]{1,2,4,3,0:T(8,128)} %bitcast.68, f32[]{:T(128)} %constant.120.clone.1), dimensions={4}, to_apply=%region_3.0 | reduce | flops 196608 | bytes 1310724 | tf_op jit(solution)/shard_map/reduce_sum | solution.py:19
  30.5 2.8 %copy.46 = f32[2,32,8,512]{1,2,3,0:T(8,128)} copy(f32[2,32,8,512]{3,2,1,0:T(8,128)S(1)} %get-tuple-element.55) | data formatting | bytes 2097152 | tf_op jit(solution)/shard_map/mul | solution.py:19
  33.3 4.0 %reduce_sum.119 = f32[2,32,8,128]{1,2,3,0:T(8,128)} reduce(f32[2,32,8,128,4]{1,2,4,3,0:T(8,128)} %bitcast.69, f32[]{:T(128)} %constant.120.clone.1), dimensions={4}, to_apply=%region_4.0 | reduce | flops 196608 | bytes 1310724 | tf_op jit(solution)/shard_map/reduce_sum | solution.py:19
  37.5 1.5 add_dynamic-update-slice_fusion.2
  40.5 2.8 %collective-permute-start = (f32[2,32,8,2]{1,2,3,0:T(8,128)S(1)}, f32[2,32,8,2]{1,2,3,0:T(8,128)S(1)}, u32[]{:S(2)}, u32[]{:S(2)}) collective-permute-start(f32[2,32,8,2]{1,2,3,0:T(8,128)S(1)} %get-tuple-element.50), channel_id=1, source_target_pairs={{0,4},{4,8},{8,12},{12,16},{16,20},{20,24},{24,28},{28,32},{32,36}... | collective-permute-start | bytes 12296 | tf_op jit(solution)/shard_map/ppermute | solution.py:14
  48.5 2.0 %gather_fusion = f32[64,2,32,128]{3,2,1,0:T(8,128)} fusion(f32[2,32,64,128]{3,1,2,0:T(8,128)S(1)} %maximum_add_fusion, s32[1024]{0:T(1024)S(1)} %pad_clamp_fusion), kind=kCustom, calls=%fused_computation | custom fusion | bytes 4194560 | tf_op jit(solution)/shard_map/jit(_take)/gather | solution.py:69
  50.5 3.1 %select_bitcast_fusion = f32[2,32,64,128]{3,1,0,2:T(8,128)} fusion(f32[64,2,32,128]{3,2,1,0:T(8,128)} %gather_fusion, pred[64]{0:T(512)(128)(4,1)S(1)} %compare_and_fusion), kind=kLoop, calls=%fused_computation.27 | loop fusion | flops 524288 | bytes 4194368 | tf_op jit(solution)/shard_map/jit(_take)/select_n | solution.py:69
  53.6 12.7 %all-to-all-start = ((f32[2,32,64,128]{3,1,0,2:T(8,128)}), f32[2,32,64,128]{3,1,0,2:T(8,128)S(1)}, u32[]{:S(2)}, u32[]{:S(2)}) async-start(f32[2,32,64,128]{3,1,0,2:T(8,128)} %select_bitcast_fusion), calls=%async_computation | async-start | bytes 4194304 | tf_op jit(solution)/shard_map/all_to_all | solution.py:70
  75.4 2.2 %mul.357 = f32[2048,4]{1,0:T(8,128)} reshape(f32[8192]{0:T(1024)S(1)} %get-tuple-element.40) | data formatting | bytes 65536 | tf_op jit(solution)/shard_map/mul | solution.py:19
  77.6 2.1 %mul.360 = f32[2048,4]{1,0:T(8,128)} reshape(f32[8192]{0:T(1024)S(1)} %get-tuple-element.42) | data formatting | bytes 65536 | tf_op jit(solution)/shard_map/mul | solution.py:19
  79.6 2.1 %mul.363 = f32[2048,4]{1,0:T(8,128)} reshape(f32[8192]{0:T(1024)S(1)} %get-tuple-element.41) | data formatting | bytes 65536 | tf_op jit(solution)/shard_map/mul | solution.py:19
  83.3 1.5 copy.62
  84.8 1.3 copy.65
  86.1 1.5 copy.66
  92.4 1.4 fusion.26
  94.1 4.6 %copy.50 = f32[2,32,64,128]{1,3,2,0:T(8,128)} copy(f32[2,32,64,128]{3,1,0,2:T(8,128)S(1)} %all-to-all-done) | data formatting | bytes 4194304 | tf_op jit(solution)/shard_map/all_to_all | solution.py:70
  98.7 40.8 %multiply_reduce_fusion.3 = (f32[2,32,2048]{1,2,0:T(8,128)}, f32[2,32,2048]{1,2,0:T(8,128)S(1)}, f32[2,32,2048]{1,2,0:T(8,128)}, f32[2,32,2048]{1,2,0:T(8,128)}) fusion(f32[2,32,1,2048,4]{1,4,3,0,2:T(4,128)} %bitcast.65, f32[2048,4]{1,0:T(8,128)S(1)} %mul.354, f32[2048,4]{1,0:T(8,128)} %mul.363, f32[2048,4]{1,0:T(8,128)} %mul.360, f32[2048,4]{1,0:T(8,128)} %mul.357), kind=kLoop, calls=%fused_computation.6 | loop fusion | flops 3670016 | bytes 4325376 | tf_op jit(solution)/shard_map/reduce_sum | solution.py:19
  139.5 2.2 %copy.51 = f32[2,32,1,2048]{3,1,2,0:T(8,128)S(1)} copy(f32[2,32,1,2048]{1,3,0,2:T(8,128)} %bitcast.73) | data formatting | bytes 1048576 | tf_op jit(solution)/shard_map/reduce_sum | solution.py:19
  141.7 2.2 %copy.53 = f32[2,32,1,2048]{3,1,2,0:T(8,128)S(1)} copy(f32[2,32,1,2048]{1,3,0,2:T(8,128)} %bitcast.72) | data formatting | bytes 1048576 | tf_op jit(solution)/shard_map/reduce_sum | solution.py:19
  143.8 3.0 %copy.55 = f32[2,32,1,2048]{3,1,2,0:T(8,128)} copy(f32[2,32,1,2048]{1,3,0,2:T(8,128)} %bitcast.71) | data formatting | bytes 1048576 | tf_op jit(solution)/shard_map/reduce_sum | solution.py:19
  146.8 1.4 copy.57
  148.2 2.4 %fusion.12 = f32[2,32,1,2048]{3,1,2,0:T(8,128)S(1)} fusion(s32[]{:T(128)S(6)} %select_n.80, f32[2,32,1,2048]{3,1,2,0:T(8,128)} %copy.57, s32[]{:T(128)S(6)} %select_n.78, f32[2,32,1,2048]{3,1,2,0:T(8,128)} %copy.55, s32[]{:T(128)S(6)} %select_n.76, f32[2,32,1,2048]{3,1,2,0:T(8,128)S(1)} %copy.53, s32[]{:T(128)S(6)} %select_n.74, f32[2,32,1,2048]{3,1,2,0:T(8,128)S(1)} %copy.51), kind=kLoop, calls=%fused_computation.55 | loop fusion | flops 917504 | bytes 2621456 | tf_op jit(solution)/shard_map/add | solution.py:37
  152.8 3.6 %multiply_reduce_fusion.7 = (f32[2,32,8,512]{3,2,1,0:T(8,128)S(1)}, f32[2,32,8,512]{3,2,1,0:T(8,128)S(1)}, f32[2,32,8,512]{3,2,1,0:T(8,128)S(1)}, f32[2,32,8,512]{3,2,1,0:T(8,128)S(1)}) fusion(f32[512,4]{0,1:T(4,128)S(1)} %copy-done.7, f32[1,32,8,512,4]{3,2,4,1,0:T(8,128)S(1)} %get-tuple-element.60, f32[1,32,8,512,4]{3,2,4,1,0:T(8,128)S(1)} %get-tuple-element.59, ...), kind=kLoop, calls=%fused_computation.17 | loop fusion | flops 8388608 | bytes 8421376 | tf_op jit(solution)/shard_map/reduce_sum | solution.py:19
  156.4 2.3 %fusion.5 = f32[2,32,8,512]{3,2,1,0:T(8,128)S(1)} fusion(s32[]{:T(128)S(6)} %select_n.88, f32[2,32,8,512]{3,2,1,0:T(8,128)S(1)} %get-tuple-element.38, s32[]{:T(128)S(6)} %select_n.86, f32[2,32,8,512]{3,2,1,0:T(8,128)S(1)} %get-tuple-element.37, s32[]{:T(128)S(6)} %select_n.84, f32[2,32,8,512]{3,2,1,0:T(8,128)S(1)} %get-tuple-element.36, s32[]{:T(128)S(6)} %select_n.82, ...), kind=kLoop, calls=%fused_computation.37 | loop fusion | flops 1835008 | bytes 5242896 | tf_op jit(solution)/shard_map/add | solution.py:37
  160.0 4.5 %pad_maximum_fusion = f32[2,32,64,512]{3,2,1,0:T(8,128)} fusion(f32[1,32,64,512]{3,2,1,0:T(8,128)S(1)} %get-tuple-element.48, f32[1,32,64,512]{3,2,1,0:T(8,128)S(1)} %get-tuple-element.47), kind=kLoop, calls=%fused_computation.2 | loop fusion | flops 2097152 | bytes 16777216 | tf_op jit(solution)/shard_map/stack | solution.py:44
  (64 shorter events, 18.9 us)
Async XLA Ops:
  37.5 1.6 copy-start
  39.1 1.2 copy-start.1
  40.3 5.0 %copy-start.5 = (f32[64,128]{1,0:T(8,128)S(1)}, f32[64,128]{1,0:T(8,128)}, u32[]{:S(2)}) copy-start(f32[64,128]{1,0:T(8,128)} %param.20) | copy-start | bytes 98308
  40.5 5.1 %collective-permute-start = (f32[2,32,8,2]{1,2,3,0:T(8,128)S(1)}, f32[2,32,8,2]{1,2,3,0:T(8,128)S(1)}, u32[]{:S(2)}, u32[]{:S(2)}) collective-permute-start(f32[2,32,8,2]{1,2,3,0:T(8,128)S(1)} %get-tuple-element.50), channel_id=1, source_target_pairs={{0,4},{4,8},{8,12},{12,16},{16,20},{20,24},{24,28},{28,32},{32,36}... | collective-permute-start | bytes 12296 | tf_op jit(solution)/shard_map/ppermute | solution.py:14
  43.2 3.2 %collective-permute-start.1 = (f32[2,32,8,2]{1,2,3,0:T(8,128)S(1)}, f32[2,32,8,2]{1,2,3,0:T(8,128)S(1)}, u32[]{:S(2)}, u32[]{:S(2)}) collective-permute-start(f32[2,32,8,2]{1,2,3,0:T(8,128)S(1)} %get-tuple-element.49), channel_id=1, source_target_pairs={{0,252},{4,0},{8,4},{12,8},{16,12},{20,16},{24,20},{28,24},{32,28}... | collective-permute-start | bytes 12296 | tf_op jit(solution)/shard_map/ppermute | solution.py:14
  46.5 1.2 copy-start.2
  53.6 20.3 %copy-start.3 = (f32[4,8192]{1,0:T(4,128)S(1)}, f32[4,8192]{1,0:T(4,128)}, u32[]{:S(2)}) copy-start(f32[4,8192]{1,0:T(4,128)} %param.24) | copy-start | bytes 393220
  53.6 40.4 %all-to-all-start = ((f32[2,32,64,128]{3,1,0,2:T(8,128)}), f32[2,32,64,128]{3,1,0,2:T(8,128)S(1)}, u32[]{:S(2)}, u32[]{:S(2)}) async-start(f32[2,32,64,128]{3,1,0,2:T(8,128)} %select_bitcast_fusion), calls=%async_computation | async-start | bytes 4194304 | tf_op jit(solution)/shard_map/all_to_all | solution.py:70
  74.3 7.4 %copy-start.4 = (f32[8,2048]{1,0:T(8,128)S(1)}, f32[8,2048]{1,0:T(8,128)}, u32[]{:S(2)}) copy-start(f32[8,2048]{1,0:T(8,128)} %param.21) | copy-start | bytes 196612
  81.9 5.7 %copy-start.6 = (f32[4,2048]{1,0:T(4,128)S(1)}, f32[4,2048]{1,0:T(4,128)}, u32[]{:S(2)}) copy-start(f32[4,2048]{1,0:T(4,128)} %param.25) | copy-start | bytes 98308
  152.1 0.7 copy-start.7
  152.1 0.7 copy-start.8
where the time goes:
time: 166 us; the launch traced here: 164 us
  other arithmetic  80.1 us (48%)
  local copies, waits for them, and re-layouts  54.1 us (33%)
  starting transfers between devices  16 us (10%)
  between operations  13.1 us (8%)
    reduce_sum x6, other arithmetic, grouped(): (fine * row).reshape(shape[:-1] + (shape[-1] // RATIO, RATIO)).sum(axis=-1)  59.5 us
    mul x16, local copies, waits for them, and re-layouts, grouped(): fine * row  23.5 us
    all_to_all x1, starting transfers between devices, body(): mine = lax.all_to_all(sent, 'ang', split_axis=2, concat_axis=3, tiled=True)  12.7 us
    reduce_sum x4, local copies, waits for them, and re-layouts, grouped(): (fine * row).reshape(shape[:-1] + (shape[-1] // RATIO, RATIO)).sum(axis=-1)  8.68 us
    add x2, other arithmetic, wrapped(): total + jnp.roll(grouped(fine, weights[index]), offsets[index], axis=-1)  4.69 us
    all_to_all x1, local copies, waits for them, and re-layouts, body(): mine = lax.all_to_all(sent, 'ang', split_axis=2, concat_axis=3, tiled=True)  4.63 us
    another operation x1, other arithmetic, rotate(): jnp.stack([field[0] * cosine - field[1] * sine, field[0] * sine + field[1...  4.46 us
    ppermute x2, starting transfers between devices, from_behind(): lax.ppermute(value, axis, [(i, (i + by) % count) for i in range(count)])  3.37 us
  transfers between devices with their start and end apart: 3, of which 2 were waited for; matrix products, arithmetic and copies ran while one was open for 13% of the time, Pallas kernels for 0%

commit v1 on v0

v1 whole, which is shorter than its diff:
```python
import functools

import jax
import jax.numpy as jnp
from jax import lax
from jax.experimental import pallas as pl
from jax.experimental.pallas import tpu as pltpu
from jax.sharding import PartitionSpec as P

STENCIL = 4
ANG = 64
ROWS = 24
PITCH = 72
NT = (((1,), (1,)), ((), ()))
F32 = jnp.float32
BF16 = jnp.bfloat16
VMEM = pl.BlockSpec(memory_space=pltpu.VMEM)
SMEM = pl.BlockSpec(memory_space=pltpu.SMEM)
ANY = pl.BlockSpec(memory_space=pl.ANY)


def halves(value):
    high = value.astype(BF16)
    return high, (value - high.astype(F32)).astype(BF16)


def iota(shape, dim):
    return lax.broadcasted_iota(jnp.int32, shape, dim)


def product(left, right):
    return lax.dot_general(left, right, NT, preferred_element_type=F32)


def send_kernel(
    incoming, own, phase, weight_top, weight_leaf, offsets, owner, message,
    fine, field, spread_own, coarse, rims, sems,
):
    ang = lax.axis_index("ang")
    box = lax.axis_index("box")
    send_body(ang, box, incoming, own, phase, weight_top, weight_leaf, offsets, owner, message,
              fine, field, spread_own, coarse, rims, sems)


def send_body(
    ang, box, incoming, own, phase, weight_top, weight_leaf, offsets, owner, message,
    fine, field, spread_own, coarse, rims, sems,
):
    get_fine = pltpu.make_async_copy(incoming, fine, sems.at[0])
    get_field = pltpu.make_async_copy(own, field, sems.at[1])
    get_fine.start()
    get_field.start()

    cosine = jnp.cos(phase[...])
    sine = jnp.sin(phase[...])
    lane = iota((64, 128), 1)
    rim_phase = jnp.where(
        (lane < 2) | (lane >= 126),
        cosine,
        jnp.where(lane < 64, pltpu.roll(sine, 2, 1), pltpu.roll(sine, 126, 1)),
    )

    top = []
    for part in range(2):
        at = iota((128, 256), 0)
        group = (iota((128, 256), 1) + 256 * part) // 4
        total = jnp.zeros((128, 256), F32)
        for o in range(STENCIL):
            hit = at == ((group + offsets[o] + 128) & 127)
            total = total + jnp.where(hit, weight_top[o : o + 1, 256 * part : 256 * part + 256], 0.0)
        top.append(jnp.concatenate(halves(total), axis=0))

    row = iota((48, 128), 0)
    inner = row % 24
    first = row < 24
    at = jnp.where(inner < 16, inner + jnp.where(first, 0, 16), inner - 16 + jnp.where(first, 32, -2))
    at = jnp.where(inner < 18, at, -100)
    group = iota((48, 128), 1) // 4
    local = weight_leaf[:, pl.ds(pl.multiple_of(ang * 128, 128), 128)]
    total = jnp.zeros((48, 128), F32)
    for o in range(STENCIL):
        total = total + jnp.where(at == group + offsets[o], local[o : o + 1, :], 0.0)
    high, low = halves(total)
    leaf = jnp.concatenate(
        [jnp.concatenate([high, high], axis=1), jnp.concatenate([low, low], axis=1)], axis=0
    )

    get_fine.wait()
    wide = iota((128, 128), 1)
    for block in range(4):
        rows = fine[block // 2, pl.ds(16 * (block % 2), 16)].reshape(128, 512)
        high, low = halves(rows)
        sums = []
        for part in range(2):
            a = high[:, 256 * part : 256 * part + 256]
            b = low[:, 256 * part : 256 * part + 256]
            y = product(a, top[part]) + product(b, top[part])
            sums.append(y[:, :128] + y[:, 128:])
        coarse[pl.ds(128 * block, 128), :] = jnp.where(
            wide < 2, sums[0], jnp.where(wide >= 126, sums[1], sums[0] + sums[1])
        )
        rims[pl.ds(128 * block, 128), :] = jnp.where(wide >= 64, sums[0], sums[1])

    srow = iota((16, 128), 0)
    slane = iota((16, 128), 1)
    pick = (
        ((srow == 2) & (slane == 0))
        | ((srow == 3) & (slane == 1))
        | ((srow == 10) & (slane == 126))
        | ((srow == 11) & (slane == 127))
    )
    pick = jnp.where(pick, 1.0, 0.0).astype(BF16)
    pick = jnp.concatenate([pick, pick], axis=1)
    rim_tiles = []
    side = iota((8, 128), 1) < 64
    for pair in range(4):
        stacked = []
        for p in (2 * pair, 2 * pair + 1):
            for c in range(2):
                stacked.append(rims[pl.ds(c * 256 + p, 32, stride=8), :])
        high, low = halves(jnp.concatenate(stacked, axis=0))
        got = product(pick, jnp.concatenate([high, low], axis=1))
        right, left = got[:8], got[8:]
        rim_tiles.append(jnp.where(side, right, pltpu.roll(left, 64, 1)))
        rim_tiles.append(jnp.where(side, pltpu.roll(right, 64, 1), left))

    get_field.wait()
    for c in range(2):
        for r in range(32):
            spread_own[pl.ds((c * 32 + r) * PITCH, 64), :] = field[c, r].astype(F32)

    half = iota((24, 128), 1) < 64
    fifth = iota((8, 128), 0) == 4
    for p in range(8):
        x = coarse[pl.ds(p, 32, stride=8), :]
        y = coarse[pl.ds(256 + p, 32, stride=8), :]
        for quad in range(2):
            highs, lows = [], []
            for child in range(4):
                b = 8 * p + 4 * quad + child
                c = cosine[b : b + 1]
                s = sine[b : b + 1]
                ox = spread_own[pl.ds(b, 32, stride=PITCH), :]
                oy = spread_own[pl.ds(32 * PITCH + b, 32, stride=PITCH), :]
                for z in (x * c - y * s + ox, x * s + y * c + oy):
                    high, low = halves(z)
                    highs.append(high)
                    lows.append(low)
            right = jnp.concatenate(
                [jnp.concatenate(highs, axis=0), jnp.concatenate(lows, axis=0)], axis=1
            )
            got = product(leaf, right)
            got = got[:48] + got[48:]
            for pair in range(2):
                a = got[:24, 128 * pair : 128 * pair + 128]
                d = got[24:, 128 * pair : 128 * pair + 128]
                for odd in range(2):
                    b = 8 * p + 4 * quad + 2 * pair + odd
                    if odd:
                        tile = jnp.where(half, pltpu.roll(a, 64, 1), d)
                    else:
                        tile = jnp.where(half, a, pltpu.roll(d, 64, 1))
                    target = owner[box, b]
                    extra = rim_tiles[p] + jnp.where(fifth, rim_phase[b : b + 1], 0.0)
                    message[target, 0:16, :] = tile[:16]
                    message[target, 16:24, :] = tile[16:] + extra


def send(incoming, own, phase, weight_top, weight_leaf, offsets, owner):
    return pl.pallas_call(
        send_kernel,
        out_shape=jax.ShapeDtypeStruct((ANG, ROWS, 128), F32),
        in_specs=[ANY, ANY, VMEM, VMEM, VMEM, SMEM, SMEM],
        out_specs=VMEM,
        scratch_shapes=SEND_SCRATCH,
        compiler_params=pltpu.CompilerParams(vmem_limit_bytes=24 * 2**20),
        name="send",
    )(incoming, own, phase, weight_top, weight_leaf, offsets, owner)


SEND_SCRATCH = [
    pltpu.VMEM((2, 32, 8, 512), F32),
    pltpu.VMEM((2, 32, 64, 128), BF16),
    pltpu.VMEM((64 * PITCH, 128), F32),
    pltpu.VMEM((512, 128), F32),
    pltpu.VMEM((512, 128), F32),
    pltpu.SemaphoreType.DMA((2,)),
]


def compact(source, block, h):
    total = None
    which = iota((8, 128), 1) // 16
    for s in range(8):
        tile = source[:, (2 * block + s // 4) * 128 : (2 * block + s // 4) * 128 + 128]
        shift = (16 * s - (32 * (s % 4) + 16 * h)) % 128
        moved = pltpu.roll(tile, shift, 1) if shift else tile
        total = moved if total is None else jnp.where(which == s, moved, total)
    return total


def table_kernel(
    phase_leaf, phase_low, weight_low, weight_leaf, offsets,
    leaf_cos, leaf_sin, low_cos, low_sin, low_weight, coef, lines,
):
    low_cos[...] = jnp.cos(phase_low[...])
    low_sin[...] = jnp.sin(phase_low[...])
    angles = phase_leaf[...]
    weights = jnp.concatenate([weight_low[...], weight_low[...]], axis=0)
    at = iota((128, 128), 0)
    lane = iota((128, 128), 1)
    for block in range(8):
        columns = []
        for h in range(2):
            angle = compact(angles, block, h)
            leaf_cos[pl.ds(8 * h, 8), pl.ds(128 * block, 128)] = jnp.cos(angle)
            leaf_sin[pl.ds(8 * h, 8), pl.ds(128 * block, 128)] = jnp.sin(angle)
            w = compact(weights, block, h)
            group = 64 * block + (lane // 16) * 8 + 4 * h + (lane % 16) // 4
            total = jnp.zeros((128, 128), F32)
            for o in range(STENCIL):
                total = total + jnp.where(at == ((group + offsets[o] + 512) & 127), w[o : o + 1], 0.0)
            columns.append(jnp.concatenate(halves(total), axis=0))
        low_weight[block] = jnp.concatenate(columns, axis=1)

    for o in range(STENCIL):
        for g in range(ANG):
            lines[pl.ds(64 * o + g, 1), :] = weight_leaf[pl.ds(o, 1), pl.ds(128 * g, 128)]
    side = iota((64, 128), 1) < 64
    for e in range(2):
        each = []
        for o in range(STENCIL):
            part = lines[pl.ds(64 * o, 64), :]
            right = pltpu.roll(jnp.broadcast_to(part[:, e : e + 1], (64, 128)), 63, 0)
            left = pltpu.roll(jnp.broadcast_to(part[:, 126 + e : 127 + e], (64, 128)), 1, 0)
            each.append(jnp.where(side, right, left))
        for m in range(5):
            total = jnp.zeros((64, 128), F32)
            for o in range(STENCIL):
                total = total + jnp.where(offsets[o] == m - 2, each[o], 0.0)
            coef[2 * m + e] = total


def tables(phase_leaf, phase_low, weight_low, weight_leaf, offsets):
    return pl.pallas_call(
        table_kernel,
        out_shape=[
            jax.ShapeDtypeStruct((16, 1024), F32),
            jax.ShapeDtypeStruct((16, 1024), F32),
            jax.ShapeDtypeStruct((64, 512), F32),
            jax.ShapeDtypeStruct((64, 512), F32),
            jax.ShapeDtypeStruct((8, 256, 256), BF16),
            jax.ShapeDtypeStruct((10, 64, 128), F32),
        ],
        in_specs=[VMEM, VMEM, VMEM, VMEM, SMEM],
        out_specs=[VMEM] * 6,
        scratch_shapes=[pltpu.VMEM((256, 128), F32)],
        compiler_params=pltpu.CompilerParams(vmem_limit_bytes=16 * 2**20),
        name="tables",
    )(phase_leaf, phase_low, weight_low, weight_leaf, offsets)


def receive_kernel(
    got, leaf_cos, leaf_sin, low_cos, low_sin, low_weight, coef, out,
    lines, added, parts, low, result, sems,
):
    side = iota((64, 128), 1) < 64
    lane = iota((64, 128), 1)

    def line(i):
        return lines[pl.ds(i, 64, stride=8), :]

    for s in range(ANG):
        lines[pl.ds(8 * s, 8), :] = got[s, 16:24, :]
    cs = line(4)

    def spread(right, left):
        right = pltpu.roll(jnp.broadcast_to(cs[:, right : right + 1], (64, 128)), 63, 0)
        left = pltpu.roll(jnp.broadcast_to(cs[:, left : left + 1], (64, 128)), 1, 0)
        return jnp.where(side, right, left)

    turned = []
    for e in range(2):
        t = line(2 + e)
        c = spread(e, 126 + e)
        s = spread(2 + e, 124 + e)
        is_x = (lane & 63) < 32
        other = jnp.where(is_x, pltpu.roll(t, 96, 1), pltpu.roll(t, 32, 1))
        turned.append(t * c + other * jnp.where(is_x, -s, s))
    e = [coef[2 * m] * turned[0] + coef[2 * m + 1] * turned[1] for m in range(5)]
    l0, l1 = line(0), line(1)
    e[1] = e[1] + jnp.where(side, 0.0, l0)
    e[2] = e[2] + jnp.where(side, l0, l1)
    e[3] = e[3] + jnp.where(side, l1, 0.0)

    def before(v):
        return pltpu.roll(v, 1, 0)

    def after(v):
        return pltpu.roll(v, 63, 0)

    def swap(v):
        return pltpu.roll(v, 64, 1)

    added[...] = jnp.zeros_like(added)
    rows = {
        0: jnp.where(side, before(e[2]) + swap(e[3]), 0.0),
        1: jnp.where(side, before(e[3]) + swap(e[4]), 0.0),
        2: jnp.where(side, before(e[4]), 0.0),
        13: jnp.where(side, 0.0, after(e[0])),
        14: jnp.where(side, 0.0, after(e[1]) + swap(e[0])),
        15: jnp.where(side, 0.0, after(e[2]) + swap(e[1])),
    }
    for i, value in rows.items():
        added[pl.ds(i, 64, stride=16), :] = value

    for block in range(8):
        tile = got[pl.ds(8 * block, 8), 0:16, :].reshape(128, 128) + added[pl.ds(128 * block, 128), :]
        flat = tile.T
        highs, lows = [], []
        for child in range(8):
            pair = []
            for h in range(2):
                x = flat[64 * h : 64 * h + 32]
                y = flat[64 * h + 32 : 64 * h + 64]
                c = leaf_cos[pl.ds(8 * h + child, 1), pl.ds(128 * block, 128)]
                s = leaf_sin[pl.ds(8 * h + child, 1), pl.ds(128 * block, 128)]
                pair.append((halves(x * c - y * s), halves(x * s + y * c)))
            for component in range(2):
                highs.append(jnp.concatenate([pair[0][component][0], pair[1][component][0]], axis=1))
                lows.append(jnp.concatenate([pair[0][component][1], pair[1][component][1]], axis=1))
        w = low_weight[block]
        y = product(jnp.concatenate(highs, axis=0), w) + product(jnp.concatenate(lows, axis=0), w)
        parts[block] = y[:, :128] + y[:, 128:]

    wide = iota((512, 128), 1)
    for t in range(4):
        here, there = parts[2 * t], parts[2 * t + 1]
        total = jnp.where(
            wide < 2,
            here + parts[(2 * t + 7) % 8],
            jnp.where(wide >= 126, there + parts[(2 * t + 2) % 8], here + there),
        )
        low[:, pl.ds(128 * t, 128)] = total

    def copies(r):
        return [pltpu.make_async_copy(result.at[c, r], out.at[c, r], sems.at[c, r]) for c in range(2)]

    def step(r, carry):
        for child in range(8):
            x = low[pl.ds(64 * child + r, 1), :]
            y = low[pl.ds(64 * child + 32 + r, 1), :]
            c = low_cos[pl.ds(8 * child, 8), :]
            s = low_sin[pl.ds(8 * child, 8), :]
            result[0, r, pl.ds(8 * child, 8), :] = x * c - y * s
            result[1, r, pl.ds(8 * child, 8), :] = x * s + y * c
        for copy in copies(r):
            copy.start()
        return carry

    lax.fori_loop(0, 32, step, 0)

    def finish(r, carry):
        for copy in copies(r):
            copy.wait()
        return carry

    lax.fori_loop(0, 32, finish, 0)


RECEIVE_SCRATCH = [
    pltpu.VMEM((512, 128), F32),
    pltpu.VMEM((1024, 128), F32),
    pltpu.VMEM((8, 512, 128), F32),
    pltpu.VMEM((512, 512), F32),
    pltpu.VMEM((2, 32, 64, 512), F32),
    pltpu.SemaphoreType.DMA((2, 32)),
]


def receive(got, ready):
    return pl.pallas_call(
        receive_kernel,
        out_shape=jax.ShapeDtypeStruct((2, 32, 64, 512), F32),
        in_specs=[VMEM] * 7,
        out_specs=ANY,
        scratch_shapes=RECEIVE_SCRATCH,
        compiler_params=pltpu.CompilerParams(vmem_limit_bytes=32 * 2**20),
        name="receive",
    )(got, *ready)


def body(
    incoming, own_field, phase_mid, phase_leaf, phase_low,
    weight_top, weight_leaf, weight_low, offsets, owner,
):
    message = send(incoming, own_field, phase_mid, weight_top, weight_leaf, offsets, owner)
    got = lax.all_to_all(message, "ang", split_axis=0, concat_axis=0, tiled=True)
    ready = tables(phase_leaf, phase_low, weight_low, weight_leaf, offsets)
    return receive(got, ready)


def solution(mesh):
    placed = (
        P(None, None, "box", "ang"),
        P(None, None, "box", "ang"),
        P("box", "ang"),
        P(("ang", "box"), None),
        P(("ang", "box"), None),
        P(None, "ang"),
        P(),
        P(),
        P(),
        P(),
    )
    return jax.shard_map(
        body,
        mesh=mesh,
        in_specs=placed,
        out_specs=P(None, None, ("ang", "box"), None),
        check_vma=False,
    )
```

time: 166 us -> 41.6 us (0.25)
  other arithmetic: 80.1 us -> 0 us
  local copies, waits for them, and re-layouts: 54.1 us -> 10.2 us
  between operations: 13.1 us -> 0.04 us
  Pallas kernels: 0 us -> 12.8 us
  waiting for transfers between devices: 1.04 us -> 7.72 us
  starting transfers between devices: 16 us -> 10.3 us
    reduce_sum x6 -> x0, other arithmetic: 59.5 us -> none  [grouped(): (fine * row).reshape(shape[:-1] + (shape[-1] // RATIO, RATIO)).sum(axis=-1)]
    mul x18 -> x0, local copies, waits for them, and re-layouts: 26.5 us -> none  [the longest x16 23.5 us: grouped(): fine * row]
    pallas_call x0 -> x3, Pallas kernels: none -> 12.8 us  [the longest x1 5.67 us: receive(): pl.pallas_call(receive_kernel, out_shape=jax.ShapeDtypeStruct((2, 32, 64,...]
    reduce_sum x4 -> x0, local copies, waits for them, and re-layouts: 8.68 us -> none  [grouped(): (fine * row).reshape(shape[:-1] + (shape[-1] // RATIO, RATIO)).sum(axis=-1)]
    unnamed x18 -> x24, local copies, waits for them, and re-layouts: 1.61 us -> 10.2 us
    all_to_all x1, waiting for transfers between devices: 0.25 us -> 7.72 us  [body(): lax.all_to_all(message, 'ang', split_axis=0, concat_axis=0, tiled=True)]
    add x6 -> x0, other arithmetic: 7.39 us -> none  [the longest x2 4.69 us: wrapped(): total + jnp.roll(grouped(fine, weights[index]), offsets[index], axis=-1)]
    all_to_all x1 -> x0, local copies, waits for them, and re-layouts: 4.63 us -> none  [body(): mine = lax.all_to_all(sent, 'ang', split_axis=2, concat_axis=3, tiled=True)]
  transfers between devices with their start and end apart: 3 -> 1, of which waited for: 2 -> 1; matrix products, arithmetic and copies ran while one was open for 13% -> 0% of each run, Pallas kernels for 0% -> 7%
where the time goes in v1:
time: 41.6 us; the launch traced here: 41.1 us
  Pallas kernels  12.8 us (31%)
  starting transfers between devices  10.3 us (25%)
  local copies, waits for them, and re-layouts  10.2 us (25%)
  waiting for transfers between devices  7.72 us (19%)
    all_to_all x1, starting transfers between devices, body(): lax.all_to_all(message, 'ang', split_axis=0, concat_axis=0, tiled=True)  10.3 us
    unnamed x24, local copies, waits for them, and re-layouts  10.2 us
    all_to_all x1, waiting for transfers between devices, body(): lax.all_to_all(message, 'ang', split_axis=0, concat_axis=0, tiled=True)  7.72 us
    pallas_call x1, Pallas kernels, receive(): pl.pallas_call(receive_kernel, out_shape=jax.ShapeDtypeStruct((2, 32, 64,...  5.67 us
    pallas_call x1, Pallas kernels, send(): pl.pallas_call(send_kernel, out_shape=jax.ShapeDtypeStruct((ANG, ROWS, 12...  4.28 us
    pallas_call x1, Pallas kernels, tables(): pl.pallas_call(table_kernel, out_shape=[jax.ShapeDtypeStruct((16, 1024),...  2.84 us
  transfers between devices with their start and end apart: 1, of which 1 were waited for; matrix products, arithmetic and copies ran while one was open for 0% of the time, Pallas kernels for 7%

profile of v1, /device:TPU:1, one launch (start us, length us, event | category | flops | bytes accessed | tf_op | source)
XLA Modules:
  0.0 41.1 jit_solution(12317625812693894723)
XLA Ops:
  0.0 0.0 copy-start
  0.0 1.2 %copy-done = f32[2,32,8,512]{3,2,1,0:T(8,128)S(1)} copy-done((f32[2,32,8,512]{3,2,1,0:T(8,128)S(1)}, f32[2,32,8,512]{3,2,1,0:T(8,128)}, u32[]{:S(2)}) %copy-start) | copy-done | bytes 1048600
  1.2 0.0 copy-start.1
  1.2 1.2 %copy-done.1 = bf16[2,32,64,128]{3,2,1,0:T(8,128)(2,1)S(1)} copy-done((bf16[2,32,64,128]{3,2,1,0:T(8,128)(2,1)S(1)}, bf16[2,32,64,128]{3,2,1,0:T(8,128)(2,1)}, u32[]{:S(2)}) %copy-start.1) | copy-done | bytes 1048600
  2.5 0.0 copy-start.2
  2.5 0.9 %copy-done.2 = f32[4,8192]{1,0:T(4,128)S(1)} copy-done((f32[4,8192]{1,0:T(4,128)S(1)}, f32[4,8192]{1,0:T(4,128)}, u32[]{:S(2)}) %copy-start.2) | copy-done | bytes 131096
  3.4 0.0 copy-start.6
  3.4 0.8 %copy-done.6 = f32[64,128]{1,0:T(8,128)S(1)} copy-done((f32[64,128]{1,0:T(8,128)S(1)}, f32[64,128]{1,0:T(8,128)}, u32[]{:S(2)}) %copy-start.6) | copy-done | bytes 32792
  4.1 0.0 copy-start.8
  4.1 0.7 %copy-done.8 = f32[4,512]{1,0:T(4,128)S(1)} copy-done((f32[4,512]{1,0:T(4,128)S(1)}, f32[4,512]{1,0:T(4,128)}, u32[]{:S(2)}) %copy-start.8) | copy-done | bytes 8216
  4.8 0.0 copy-start.9
  4.8 0.7 %copy-done.9 = s32[4]{0:T(128)S(1)} copy-done((s32[4]{0:T(128)S(1)}, s32[4]{0:T(128)}, u32[]{:S(2)}) %copy-start.9) | copy-done | bytes 40
  5.5 0.0 copy-start.11
  5.5 0.7 %copy-done.11 = s32[4,64]{1,0:T(4,128)S(1)} copy-done((s32[4,64]{1,0:T(4,128)S(1)}, s32[4,64]{1,0:T(4,128)}, u32[]{:S(2)}) %copy-start.11) | copy-done | bytes 1048
  6.1 4.3 %send.1 = f32[64,24,128]{2,1,0:T(8,128)} custom-call(f32[2,32,8,512]{3,2,1,0:T(8,128)S(1)} %copy-done, bf16[2,32,64,128]{3,2,1,0:T(8,128)(2,1)S(1)} %copy-done.1, f32[64,128]{1,0:T(8,128)S(1)} %copy-done.6, f32[4,512]{1,0:T(4,128)S(1)} %copy-done.8, f32[4,8192]{1,0:T(4,128)S(1)} %copy-done.2, s32[4]{0:T(128)S(1)} %copy-done.9, s32[4,64]{1,0:T(4,128)S(1)} %copy-done.11), custom_call_target="tpu_custom_call" | custom-call | tf_op jit(solution)/shard_map/send/pallas_call | solution.py:170
  10.4 10.3 %all-to-all-start = ((f32[64,24,128]{2,1,0:T(8,128)}), f32[64,24,128]{2,1,0:T(8,128)S(1)}, u32[]{:S(2)}, u32[]{:S(2)}) async-start(f32[64,24,128]{2,1,0:T(8,128)} %send.1), calls=%async_computation | async-start | bytes 1572864 | tf_op jit(solution)/shard_map/all_to_all | solution.py:398
  20.8 0.0 copy-start.3
  20.8 0.9 %copy-done.3 = f32[4,8192]{1,0:T(4,128)S(1)} copy-done((f32[4,8192]{1,0:T(4,128)S(1)}, f32[4,8192]{1,0:T(4,128)}, u32[]{:S(2)}) %copy-start.3) | copy-done | bytes 131096
  21.7 0.0 copy-start.4
  21.7 0.9 %copy-done.4 = f32[64,512]{1,0:T(8,128)S(1)} copy-done((f32[64,512]{1,0:T(8,128)S(1)}, f32[64,512]{1,0:T(8,128)}, u32[]{:S(2)}) %copy-start.4) | copy-done | bytes 131096
  22.6 0.0 copy-start.5
  22.6 0.8 %copy-done.5 = f32[8,2048]{1,0:T(8,128)S(1)} copy-done((f32[8,2048]{1,0:T(8,128)S(1)}, f32[8,2048]{1,0:T(8,128)}, u32[]{:S(2)}) %copy-start.5) | copy-done | bytes 65560
  23.4 0.0 copy-start.7
  23.4 0.8 %copy-done.7 = f32[4,2048]{1,0:T(4,128)S(1)} copy-done((f32[4,2048]{1,0:T(4,128)S(1)}, f32[4,2048]{1,0:T(4,128)}, u32[]{:S(2)}) %copy-start.7) | copy-done | bytes 32792
  24.2 0.0 copy-start.10
  24.2 0.7 %copy-done.10 = s32[4]{0:T(128)S(1)} copy-done((s32[4]{0:T(128)S(1)}, s32[4]{0:T(128)}, u32[]{:S(2)}) %copy-start.10) | copy-done | bytes 40
  24.9 2.8 %tables.1 = (f32[16,1024]{1,0:T(8,128)S(1)}, f32[16,1024]{1,0:T(8,128)S(1)}, f32[64,512]{1,0:T(8,128)S(1)}, f32[64,512]{1,0:T(8,128)S(1)}, bf16[8,256,256]{2,1,0:T(8,128)(2,1)S(1)}, /*index=5*/f32[10,64,128]{2,1,0:T(8,128)S(1)}) custom-call(f32[8,2048]{1,0:T(8,128)S(1)} %copy-done.5, f32[64,512]{1,0:T(8,128)S(1)} %copy-done.4, f32[4,2048]{1,0:T(4,128)S(1)} %copy-done.7, ...), custom_call_target="tpu_custom_call" | custom-call | tf_op jit(solution)/shard_map/tables/pallas_call | solution.py:245
  27.7 7.7 %all-to-all-done.got = f32[64,24,128]{2,1,0:T(8,128)S(1)} async-done(((f32[64,24,128]{2,1,0:T(8,128)}), f32[64,24,128]{2,1,0:T(8,128)S(1)}, u32[]{:S(2)}, u32[]{:S(2)}) %all-to-all-start) | async-done | bytes 786464 | tf_op jit(solution)/shard_map/all_to_all | solution.py:398
  35.4 5.7 %receive.1 = f32[2,32,64,512]{3,2,1,0:T(8,128)} custom-call(f32[64,24,128]{2,1,0:T(8,128)S(1)} %all-to-all-done.got, f32[16,1024]{1,0:T(8,128)S(1)} %get-tuple-element.11.leaf_cos, f32[16,1024]{1,0:T(8,128)S(1)} %get-tuple-element.12.leaf_sin, f32[64,512]{1,0:T(8,128)S(1)} %get-tuple-element.13.low_cos, f32[64,512]{1,0:T(8,128)S(1)} %get-tuple-element.14.low_sin, ...), custom_call_target="tpu_custom_call" | custom-call | tf_op jit(solution)/shard_map/receive/pallas_call | solution.py:382
Async XLA Ops:
  0.0 1.2 %copy-start = (f32[2,32,8,512]{3,2,1,0:T(8,128)S(1)}, f32[2,32,8,512]{3,2,1,0:T(8,128)}, u32[]{:S(2)}) copy-start(f32[2,32,8,512]{3,2,1,0:T(8,128)} %incoming.1) | copy-start | bytes 3145732
  1.2 1.2 %copy-start.1 = (bf16[2,32,64,128]{3,2,1,0:T(8,128)(2,1)S(1)}, bf16[2,32,64,128]{3,2,1,0:T(8,128)(2,1)}, u32[]{:S(2)}) copy-start(bf16[2,32,64,128]{3,2,1,0:T(8,128)(2,1)} %own.1) | copy-start | bytes 3145732
  2.5 0.9 %copy-start.2 = (f32[4,8192]{1,0:T(4,128)S(1)}, f32[4,8192]{1,0:T(4,128)}, u32[]{:S(2)}) copy-start(f32[4,8192]{1,0:T(4,128)} %weight_leaf.3) | copy-start | bytes 393220
  3.4 0.8 %copy-start.6 = (f32[64,128]{1,0:T(8,128)S(1)}, f32[64,128]{1,0:T(8,128)}, u32[]{:S(2)}) copy-start(f32[64,128]{1,0:T(8,128)} %phase.1) | copy-start | bytes 98308
  4.1 0.7 %copy-start.8 = (f32[4,512]{1,0:T(4,128)S(1)}, f32[4,512]{1,0:T(4,128)}, u32[]{:S(2)}) copy-start(f32[4,512]{1,0:T(4,128)} %weight_top.1) | copy-start | bytes 24580
  4.8 0.7 %copy-start.9 = (s32[4]{0:T(128)S(1)}, s32[4]{0:T(128)}, u32[]{:S(2)}) copy-start(s32[4]{0:T(128)} %offsets.3) | copy-start | bytes 52
  5.5 0.7 %copy-start.11 = (s32[4,64]{1,0:T(4,128)S(1)}, s32[4,64]{1,0:T(4,128)}, u32[]{:S(2)}) copy-start(s32[4,64]{1,0:T(4,128)} %owner.1) | copy-start | bytes 3076
  10.4 25.0 %all-to-all-start = ((f32[64,24,128]{2,1,0:T(8,128)}), f32[64,24,128]{2,1,0:T(8,128)S(1)}, u32[]{:S(2)}, u32[]{:S(2)}) async-start(f32[64,24,128]{2,1,0:T(8,128)} %send.1), calls=%async_computation | async-start | bytes 1572864 | tf_op jit(solution)/shard_map/all_to_all | solution.py:398
  20.8 0.9 %copy-start.3 = (f32[4,8192]{1,0:T(4,128)S(1)}, f32[4,8192]{1,0:T(4,128)}, u32[]{:S(2)}) copy-start(f32[4,8192]{1,0:T(4,128)} %weight_leaf.3) | copy-start | bytes 393220
  21.7 0.9 %copy-start.4 = (f32[64,512]{1,0:T(8,128)S(1)}, f32[64,512]{1,0:T(8,128)}, u32[]{:S(2)}) copy-start(f32[64,512]{1,0:T(8,128)} %phase_low.1) | copy-start | bytes 393220
  22.6 0.8 %copy-start.5 = (f32[8,2048]{1,0:T(8,128)S(1)}, f32[8,2048]{1,0:T(8,128)}, u32[]{:S(2)}) copy-start(f32[8,2048]{1,0:T(8,128)} %phase_leaf.1) | copy-start | bytes 196612
  23.4 0.8 %copy-start.7 = (f32[4,2048]{1,0:T(4,128)S(1)}, f32[4,2048]{1,0:T(4,128)}, u32[]{:S(2)}) copy-start(f32[4,2048]{1,0:T(4,128)} %weight_low.1) | copy-start | bytes 98308
  24.2 0.7 %copy-start.10 = (s32[4]{0:T(128)S(1)}, s32[4]{0:T(128)}, u32[]{:S(2)}) copy-start(s32[4]{0:T(128)} %offsets.3) | copy-start | bytes 52

commit v2 on v1

--- a/solution.py
+++ b/solution.py
@@ -9,14 +9,14 @@
 
 STENCIL = 4
 ANG = 64
-ROWS = 24
+ROWS = 21
 PITCH = 72
 NT = (((1,), (1,)), ((), ()))
 F32 = jnp.float32
 BF16 = jnp.bfloat16
 VMEM = pl.BlockSpec(memory_space=pltpu.VMEM)
 SMEM = pl.BlockSpec(memory_space=pltpu.SMEM)
-ANY = pl.BlockSpec(memory_space=pl.ANY)
+HBM = pl.BlockSpec(memory_space=pltpu.HBM)
 
 
 def halves(value):
@@ -33,24 +33,32 @@
 
 
 def send_kernel(
-    incoming, own, phase, weight_top, weight_leaf, offsets, owner, message,
-    fine, field, spread_own, coarse, rims, sems,
+    incoming, own, all_phase, all_top, all_leaf, all_offsets, all_owner, message,
+    fine, field, phase, weight_top, local, offsets, owner, spread_own, coarse, rims, sems,
 ):
     ang = lax.axis_index("ang")
     box = lax.axis_index("box")
-    send_body(ang, box, incoming, own, phase, weight_top, weight_leaf, offsets, owner, message,
-              fine, field, spread_own, coarse, rims, sems)
-
-
-def send_body(
-    ang, box, incoming, own, phase, weight_top, weight_leaf, offsets, owner, message,
-    fine, field, spread_own, coarse, rims, sems,
-):
-    get_fine = pltpu.make_async_copy(incoming, fine, sems.at[0])
-    get_field = pltpu.make_async_copy(own, field, sems.at[1])
-    get_fine.start()
-    get_field.start()
-
+    small = [
+        pltpu.make_async_copy(source, target, sems.at[i])
+        for i, (source, target) in enumerate(
+            (
+                (all_phase, phase),
+                (all_offsets, offsets),
+                (all_top, weight_top),
+                (all_leaf.at[:, pl.ds(pl.multiple_of(ang * 128, 128), 128)], local),
+                (all_owner, owner),
+            )
+        )
+    ]
+    get_fine = [
+        pltpu.make_async_copy(incoming.at[i // 2, pl.ds(16 * (i % 2), 16)], fine.at[i], sems.at[5 + i])
+        for i in range(4)
+    ]
+    get_field = [pltpu.make_async_copy(own.at[c], field.at[c], sems.at[9 + c]) for c in range(2)]
+    for copy in small + get_fine + get_field:
+        copy.start()
+
+    small[0].wait()
     cosine = jnp.cos(phase[...])
     sine = jnp.sin(phase[...])
     lane = iota((64, 128), 1)
@@ -60,6 +68,8 @@
         jnp.where(lane < 64, pltpu.roll(sine, 2, 1), pltpu.roll(sine, 126, 1)),
     )
 
+    small[1].wait()
+    small[2].wait()
     top = []
     for part in range(2):
         at = iota((128, 256), 0)
@@ -76,7 +86,7 @@
     at = jnp.where(inner < 16, inner + jnp.where(first, 0, 16), inner - 16 + jnp.where(first, 32, -2))
     at = jnp.where(inner < 18, at, -100)
     group = iota((48, 128), 1) // 4
-    local = weight_leaf[:, pl.ds(pl.multiple_of(ang * 128, 128), 128)]
+    small[3].wait()
     total = jnp.zeros((48, 128), F32)
     for o in range(STENCIL):
         total = total + jnp.where(at == group + offsets[o], local[o : o + 1, :], 0.0)
@@ -85,10 +95,10 @@
         [jnp.concatenate([high, high], axis=1), jnp.concatenate([low, low], axis=1)], axis=0
     )
 
-    get_fine.wait()
     wide = iota((128, 128), 1)
     for block in range(4):
-        rows = fine[block // 2, pl.ds(16 * (block % 2), 16)].reshape(128, 512)
+        get_fine[block].wait()
+        rows = fine[block].reshape(128, 512)
         high, low = halves(rows)
         sums = []
         for part in range(2):
@@ -124,11 +134,12 @@
         rim_tiles.append(jnp.where(side, right, pltpu.roll(left, 64, 1)))
         rim_tiles.append(jnp.where(side, pltpu.roll(right, 64, 1), left))
 
-    get_field.wait()
     for c in range(2):
+        get_field[c].wait()
         for r in range(32):
             spread_own[pl.ds((c * 32 + r) * PITCH, 64), :] = field[c, r].astype(F32)
 
+    small[4].wait()
     half = iota((24, 128), 1) < 64
     fifth = iota((8, 128), 0) == 4
     for p in range(8):
@@ -160,17 +171,17 @@
                         tile = jnp.where(half, pltpu.roll(a, 64, 1), d)
                     else:
                         tile = jnp.where(half, a, pltpu.roll(d, 64, 1))
-                    target = owner[box, b]
+                    target = owner[box, b] * ROWS
                     extra = rim_tiles[p] + jnp.where(fifth, rim_phase[b : b + 1], 0.0)
-                    message[target, 0:16, :] = tile[:16]
-                    message[target, 16:24, :] = tile[16:] + extra
+                    message[pl.ds(target, 16), :] = tile[:16]
+                    message[pl.ds(target + 16, 5), :] = (tile[16:] + extra)[:5]
 
 
 def send(incoming, own, phase, weight_top, weight_leaf, offsets, owner):
     return pl.pallas_call(
         send_kernel,
-        out_shape=jax.ShapeDtypeStruct((ANG, ROWS, 128), F32),
-        in_specs=[ANY, ANY, VMEM, VMEM, VMEM, SMEM, SMEM],
+        out_shape=jax.ShapeDtypeStruct((ANG * ROWS, 128), F32),
+        in_specs=[HBM] * 7,
         out_specs=VMEM,
         scratch_shapes=SEND_SCRATCH,
         compiler_params=pltpu.CompilerParams(vmem_limit_bytes=24 * 2**20),
@@ -179,12 +190,17 @@
 
 
 SEND_SCRATCH = [
-    pltpu.VMEM((2, 32, 8, 512), F32),
+    pltpu.VMEM((4, 16, 8, 512), F32),
     pltpu.VMEM((2, 32, 64, 128), BF16),
+    pltpu.VMEM((64, 128), F32),
+    pltpu.VMEM((4, 512), F32),
+    pltpu.VMEM((4, 128), F32),
+    pltpu.SMEM((4,), jnp.int32),
+    pltpu.SMEM((4, 64), jnp.int32),
     pltpu.VMEM((64 * PITCH, 128), F32),
     pltpu.VMEM((512, 128), F32),
     pltpu.VMEM((512, 128), F32),
-    pltpu.SemaphoreType.DMA((2,)),
+    pltpu.SemaphoreType.DMA((11,)),
 ]
 
 
@@ -271,7 +287,7 @@
         return lines[pl.ds(i, 64, stride=8), :]
 
     for s in range(ANG):
-        lines[pl.ds(8 * s, 8), :] = got[s, 16:24, :]
+        lines[pl.ds(8 * s, 5), :] = got[pl.ds(ROWS * s + 16, 5), :]
     cs = line(4)
 
     def spread(right, left):
@@ -315,7 +331,8 @@
         added[pl.ds(i, 64, stride=16), :] = value
 
     for block in range(8):
-        tile = got[pl.ds(8 * block, 8), 0:16, :].reshape(128, 128) + added[pl.ds(128 * block, 128), :]
+        tile = jnp.concatenate([got[pl.ds(ROWS * (8 * block + s), 16), :] for s in range(8)], axis=0)
+        tile = tile + added[pl.ds(128 * block, 128), :]
         flat = tile.T
         highs, lows = [], []
         for child in range(8):
@@ -383,7 +400,7 @@
         receive_kernel,
         out_shape=jax.ShapeDtypeStruct((2, 32, 64, 512), F32),
         in_specs=[VMEM] * 7,
-        out_specs=ANY,
+        out_specs=HBM,
         scratch_shapes=RECEIVE_SCRATCH,
         compiler_params=pltpu.CompilerParams(vmem_limit_bytes=32 * 2**20),
         name="receive",
@@ -394,8 +411,17 @@
     incoming, own_field, phase_mid, phase_leaf, phase_low,
     weight_top, weight_leaf, weight_low, offsets, owner,
 ):
+    incoming, own_field, phase_mid, phase_leaf, phase_low, weight_top, weight_leaf, weight_low, offsets, owner = (
+        pltpu.with_memory_space_constraint(value, pltpu.HBM)
+        for value in (
+            incoming, own_field, phase_mid, phase_leaf, phase_low,
+            weight_top, weight_leaf, weight_low, offsets, owner,
+        )
+    )
     message = send(incoming, own_field, phase_mid, weight_top, weight_leaf, offsets, owner)
+    message = message.reshape(ANG, 1, ROWS * 128)
     got = lax.all_to_all(message, "ang", split_axis=0, concat_axis=0, tiled=True)
+    got = got.reshape(ANG * ROWS, 128)
     ready = tables(phase_leaf, phase_low, weight_low, weight_leaf, offsets)
     return receive(got, ready)
 

time: 41.6 us -> 34.7 us (0.83)
  local copies, waits for them, and re-layouts: 10.2 us -> 0 us
  waiting for transfers between devices: 7.72 us -> 10.4 us
  Pallas kernels: 12.8 us -> 13.7 us
    unnamed x24 -> x0, local copies, waits for them, and re-layouts: 10.2 us -> none
    all_to_all x1, waiting for transfers between devices: 7.72 us -> 10.4 us  [body(): lax.all_to_all(message, 'ang', split_axis=0, concat_axis=0, tiled=True)]
    pallas_call x1, Pallas kernels: 2.84 us -> 3.33 us  [tables(): pl.pallas_call(table_kernel, out_shape=[jax.ShapeDtypeStruct((16, 1024),...]
    pallas_call x1, Pallas kernels: 4.28 us -> 4.73 us  [send(): pl.pallas_call(send_kernel, out_shape=jax.ShapeDtypeStruct((ANG * ROWS, 1...]
  transfers between devices with their start and end apart: 1 -> 1, of which waited for: 1 -> 1; matrix products, arithmetic and copies ran while one was open for 0% -> 0% of each run, Pallas kernels for 7% -> 10%
where the time goes in v2:
time: 34.7 us; the launch traced here: 34.5 us
  Pallas kernels  13.7 us (39%)
  waiting for transfers between devices  10.4 us (30%)
  starting transfers between devices  10.3 us (30%)
    all_to_all x1, waiting for transfers between devices, body(): lax.all_to_all(message, 'ang', split_axis=0, concat_axis=0, tiled=True)  10.4 us
    all_to_all x1, starting transfers between devices, body(): lax.all_to_all(message, 'ang', split_axis=0, concat_axis=0, tiled=True)  10.3 us
    pallas_call x1, Pallas kernels, receive(): pl.pallas_call(receive_kernel, out_shape=jax.ShapeDtypeStruct((2, 32, 64,...  5.67 us
    pallas_call x1, Pallas kernels, send(): pl.pallas_call(send_kernel, out_shape=jax.ShapeDtypeStruct((ANG * ROWS, 1...  4.73 us
    pallas_call x1, Pallas kernels, tables(): pl.pallas_call(table_kernel, out_shape=[jax.ShapeDtypeStruct((16, 1024),...  3.33 us
  transfers between devices with their start and end apart: 1, of which 1 were waited for; matrix products, arithmetic and copies ran while one was open for 0% of the time, Pallas kernels for 10%

profile of v2, /device:TPU:1, one launch (start us, length us, event | category | flops | bytes accessed | tf_op | source)
XLA Modules:
  0.0 34.5 jit_solution(17060112176987392644)
XLA Ops:
  0.0 4.7 %send.1 = f32[1344,128]{1,0:T(8,128)} custom-call(f32[2,32,8,512]{3,2,1,0:T(8,128)} %incoming.1, bf16[2,32,64,128]{3,2,1,0:T(8,128)(2,1)} %own.1, f32[64,128]{1,0:T(8,128)} %all_phase.1, f32[4,512]{1,0:T(4,128)} %all_top.1, f32[4,8192]{1,0:T(4,128)} %weight_leaf.1, s32[4]{0:T(128)} %offsets.1, s32[4,64]{1,0:T(4,128)} %all_owner.1), custom_call_target="tpu_custom_call" | custom-call | tf_op jit(solution)/shard_map/send/pallas_call | solution.py:181
  4.7 10.3 %all-to-all-start = ((f32[64,1,2688]{2,1,0:T(1,128)}), f32[64,1,2688]{2,1,0:T(1,128)S(1)}, u32[]{:S(2)}, u32[]{:S(2)}) async-start(f32[64,1,2688]{2,1,0:T(1,128)} %bitcast), calls=%async_computation | async-start | bytes 1376256 | tf_op jit(solution)/shard_map/all_to_all | solution.py:423
  15.1 3.3 %tables.1 = (f32[16,1024]{1,0:T(8,128)S(1)}, f32[16,1024]{1,0:T(8,128)S(1)}, f32[64,512]{1,0:T(8,128)S(1)}, f32[64,512]{1,0:T(8,128)S(1)}, bf16[8,256,256]{2,1,0:T(8,128)(2,1)S(1)}, /*index=5*/f32[10,64,128]{2,1,0:T(8,128)S(1)}) custom-call(f32[8,2048]{1,0:T(8,128)} %phase_leaf.1, f32[64,512]{1,0:T(8,128)} %phase_low.1, f32[4,2048]{1,0:T(4,128)} %weight_low.1, ...), custom_call_target="tpu_custom_call" | custom-call | tf_op jit(solution)/shard_map/tables/pallas_call | solution.py:261
  18.4 10.4 %all-to-all-done = f32[64,1,2688]{2,1,0:T(1,128)S(1)} async-done(((f32[64,1,2688]{2,1,0:T(1,128)}), f32[64,1,2688]{2,1,0:T(1,128)S(1)}, u32[]{:S(2)}, u32[]{:S(2)}) %all-to-all-start) | async-done | bytes 688160 | tf_op jit(solution)/shard_map/all_to_all | solution.py:423
  28.8 5.7 %receive.1 = f32[2,32,64,512]{3,2,1,0:T(8,128)} custom-call(f32[1344,128]{1,0:T(8,128)S(1)} %bitcast.2, f32[16,1024]{1,0:T(8,128)S(1)} %get-tuple-element.11.leaf_cos, f32[16,1024]{1,0:T(8,128)S(1)} %get-tuple-element.12.leaf_sin, f32[64,512]{1,0:T(8,128)S(1)} %get-tuple-element.13.low_cos, f32[64,512]{1,0:T(8,128)S(1)} %get-tuple-element.14.low_sin, ...), custom_call_target="tpu_custom_call" | custom-call | tf_op jit(solution)/shard_map/receive/pallas_call | solution.py:399
Async XLA Ops:
  4.7 24.1 %all-to-all-start = ((f32[64,1,2688]{2,1,0:T(1,128)}), f32[64,1,2688]{2,1,0:T(1,128)S(1)}, u32[]{:S(2)}, u32[]{:S(2)}) async-start(f32[64,1,2688]{2,1,0:T(1,128)} %bitcast), calls=%async_computation | async-start | bytes 1376256 | tf_op jit(solution)/shard_map/all_to_all | solution.py:423

commit v3 on v2

--- a/solution.py
+++ b/solution.py
@@ -11,6 +11,9 @@
 ANG = 64
 ROWS = 21
 PITCH = 72
+COUNT = 16
+PER = 16
+CHUNK = 16
 NT = (((1,), (1,)), ((), ()))
 F32 = jnp.float32
 BF16 = jnp.bfloat16
@@ -26,6 +29,42 @@
 
 def iota(shape, dim):
     return lax.broadcasted_iota(jnp.int32, shape, dim)
+
+
+def turn(angle):
+    count = jnp.floor(angle * 0.6366197723675814 + 0.5)
+    rest = angle - count * 1.5703125
+    rest = rest - count * 4.837512969970703e-4
+    rest = rest - count * 7.549789954891e-8
+    square = rest * rest
+    sine = ((-1.9515295891e-4 * square + 8.3321608736e-3) * square - 1.6666654611e-1) * square * rest + rest
+    cosine = ((2.443315711809948e-5 * square - 1.388731625493765e-3) * square + 4.166664568298827e-2) * square
+    cosine = cosine * square - 0.5 * square + 1.0
+    quarter = count.astype(jnp.int32)
+    odd = (quarter & 1) == 1
+    first = jnp.where(odd, sine, cosine)
+    second = jnp.where(odd, cosine, sine)
+    return (
+        jnp.where(((quarter + 1) & 2) == 2, -first, first),
+        jnp.where((quarter & 2) == 2, -second, second),
+    )
+
+
+def window(hits, weights):
+    total = None
+    for o in range(STENCIL):
+        term = jnp.where(hits[o], weights[o], 0.0)
+        total = term if total is None else total + term
+    return halves(total)
+
+
+def placed(piece, start):
+    begin = (start - 8) % 128
+    zero = jnp.zeros((80, 128), BF16)
+    if begin + 48 <= 128:
+        return jnp.concatenate([zero[:begin], piece, zero[begin:]], axis=0)
+    over = begin + 48 - 128
+    return jnp.concatenate([piece[48 - over :], zero, piece[: 48 - over]], axis=0)
 
 
 def product(left, right):
@@ -59,8 +98,7 @@
         copy.start()
 
     small[0].wait()
-    cosine = jnp.cos(phase[...])
-    sine = jnp.sin(phase[...])
+    cosine, sine = turn(phase[...])
     lane = iota((64, 128), 1)
     rim_phase = jnp.where(
         (lane < 2) | (lane >= 126),
@@ -70,27 +108,27 @@
 
     small[1].wait()
     small[2].wait()
+    apart = iota((48, 128), 0) - 8 - iota((48, 128), 1) // 4
+    hits = [apart == offsets[o] for o in range(STENCIL)]
     top = []
     for part in range(2):
-        at = iota((128, 256), 0)
-        group = (iota((128, 256), 1) + 256 * part) // 4
-        total = jnp.zeros((128, 256), F32)
-        for o in range(STENCIL):
-            hit = at == ((group + offsets[o] + 128) & 127)
-            total = total + jnp.where(hit, weight_top[o : o + 1, 256 * part : 256 * part + 256], 0.0)
-        top.append(jnp.concatenate(halves(total), axis=0))
+        highs, lows = [], []
+        for k in (2 * part, 2 * part + 1):
+            high, low = window(hits, [weight_top[o : o + 1, 128 * k : 128 * k + 128] for o in range(STENCIL)])
+            highs.append(placed(high, 32 * k))
+            lows.append(placed(low, 32 * k))
+        top.append(jnp.concatenate([jnp.concatenate(highs, axis=1), jnp.concatenate(lows, axis=1)], axis=0))
 
     row = iota((48, 128), 0)
     inner = row % 24
     first = row < 24
     at = jnp.where(inner < 16, inner + jnp.where(first, 0, 16), inner - 16 + jnp.where(first, 32, -2))
     at = jnp.where(inner < 18, at, -100)
-    group = iota((48, 128), 1) // 4
+    apart = at - iota((48, 128), 1) // 4
     small[3].wait()
-    total = jnp.zeros((48, 128), F32)
-    for o in range(STENCIL):
-        total = total + jnp.where(at == group + offsets[o], local[o : o + 1, :], 0.0)
-    high, low = halves(total)
+    high, low = window(
+        [apart == offsets[o] for o in range(STENCIL)], [local[o : o + 1, :] for o in range(STENCIL)]
+    )
     leaf = jnp.concatenate(
         [jnp.concatenate([high, high], axis=1), jnp.concatenate([low, low], axis=1)], axis=0
     )
@@ -204,39 +242,34 @@
 ]
 
 
-def compact(source, block, h):
-    total = None
-    which = iota((8, 128), 1) // 16
-    for s in range(8):
-        tile = source[:, (2 * block + s // 4) * 128 : (2 * block + s // 4) * 128 + 128]
-        shift = (16 * s - (32 * (s % 4) + 16 * h)) % 128
-        moved = pltpu.roll(tile, shift, 1) if shift else tile
-        total = moved if total is None else jnp.where(which == s, moved, total)
-    return total
-
-
 def table_kernel(
     phase_leaf, phase_low, weight_low, weight_leaf, offsets,
     leaf_cos, leaf_sin, low_cos, low_sin, low_weight, coef, lines,
 ):
-    low_cos[...] = jnp.cos(phase_low[...])
-    low_sin[...] = jnp.sin(phase_low[...])
-    angles = phase_leaf[...]
-    weights = jnp.concatenate([weight_low[...], weight_low[...]], axis=0)
-    at = iota((128, 128), 0)
-    lane = iota((128, 128), 1)
+    low_cos[...], low_sin[...] = turn(phase_low[...])
+    row, column = iota((256, 256), 0), iota((256, 256), 1)
+    order = jnp.where(column == (row % 8) * 32 + (row // 128) * 16 + (row % 128) // 8, 1.0, 0.0).astype(BF16)
+    stacked = []
+    for block in range(8):
+        stacked.append(phase_leaf[:, 256 * block : 256 * block + 256])
+        stacked.append(weight_low[:, 256 * block : 256 * block + 256])
+        stacked.append(weight_low[:, 256 * block : 256 * block + 256])
+    stacked = jnp.concatenate(stacked, axis=0)
+    high, rest = stacked.astype(BF16), stacked
+    rest = rest - high.astype(F32)
+    middle = rest.astype(BF16)
+    low = (rest - middle.astype(F32)).astype(BF16)
+    sorted_ = product(high, order) + product(middle, order) + product(low, order)
+    at, lane = iota((128, 128), 0), iota((128, 128), 1)
     for block in range(8):
         columns = []
         for h in range(2):
-            angle = compact(angles, block, h)
-            leaf_cos[pl.ds(8 * h, 8), pl.ds(128 * block, 128)] = jnp.cos(angle)
-            leaf_sin[pl.ds(8 * h, 8), pl.ds(128 * block, 128)] = jnp.sin(angle)
-            w = compact(weights, block, h)
-            group = 64 * block + (lane // 16) * 8 + 4 * h + (lane % 16) // 4
-            total = jnp.zeros((128, 128), F32)
-            for o in range(STENCIL):
-                total = total + jnp.where(at == ((group + offsets[o] + 512) & 127), w[o : o + 1], 0.0)
-            columns.append(jnp.concatenate(halves(total), axis=0))
+            part = sorted_[16 * block : 16 * block + 16, 128 * h : 128 * h + 128]
+            to = pl.ds(128 * block, 128)
+            leaf_cos[pl.ds(8 * h, 8), to], leaf_sin[pl.ds(8 * h, 8), to] = turn(part[:8])
+            apart = (at - (64 * block + (lane % 8) * 8 + 4 * h + lane // 32)) & 127
+            hits = [apart == (offsets[o] & 127) for o in range(STENCIL)]
+            columns.append(jnp.concatenate(window(hits, [part[8 + o : 9 + o] for o in range(STENCIL)]), axis=0))
         low_weight[block] = jnp.concatenate(columns, axis=1)
 
     for o in range(STENCIL):
@@ -278,16 +311,14 @@
 
 def receive_kernel(
     got, leaf_cos, leaf_sin, low_cos, low_sin, low_weight, coef, out,
-    lines, added, parts, low, result, sems,
+    flat, parts, low, result, sems,
 ):
     side = iota((64, 128), 1) < 64
     lane = iota((64, 128), 1)
 
     def line(i):
-        return lines[pl.ds(i, 64, stride=8), :]
-
-    for s in range(ANG):
-        lines[pl.ds(8 * s, 5), :] = got[pl.ds(ROWS * s + 16, 5), :]
+        return got[pl.ds(16 + i, 64, stride=ROWS), :]
+
     cs = line(4)
 
     def spread(right, left):
@@ -318,7 +349,6 @@
     def swap(v):
         return pltpu.roll(v, 64, 1)
 
-    added[...] = jnp.zeros_like(added)
     rows = {
         0: jnp.where(side, before(e[2]) + swap(e[3]), 0.0),
         1: jnp.where(side, before(e[3]) + swap(e[4]), 0.0),
@@ -327,71 +357,79 @@
         14: jnp.where(side, 0.0, after(e[1]) + swap(e[0])),
         15: jnp.where(side, 0.0, after(e[2]) + swap(e[1])),
     }
-    for i, value in rows.items():
-        added[pl.ds(i, 64, stride=16), :] = value
-
     for block in range(8):
-        tile = jnp.concatenate([got[pl.ds(ROWS * (8 * block + s), 16), :] for s in range(8)], axis=0)
-        tile = tile + added[pl.ds(128 * block, 128), :]
-        flat = tile.T
-        highs, lows = [], []
+        tiles = []
+        for i in range(16):
+            tile = got[pl.ds(8 * ROWS * block + i, 8, stride=ROWS), :]
+            if i in rows:
+                tile = tile + rows[i][8 * block : 8 * block + 8]
+            tiles.append(tile)
+        flat[block] = jnp.concatenate(tiles, axis=0).T
+
+    def anterpolate(block, start, count):
+        at = pl.ds(128 * block, 128)
+        rows = []
         for child in range(8):
             pair = []
             for h in range(2):
-                x = flat[64 * h : 64 * h + 32]
-                y = flat[64 * h + 32 : 64 * h + 64]
-                c = leaf_cos[pl.ds(8 * h + child, 1), pl.ds(128 * block, 128)]
-                s = leaf_sin[pl.ds(8 * h + child, 1), pl.ds(128 * block, 128)]
-                pair.append((halves(x * c - y * s), halves(x * s + y * c)))
+                x = flat[block, pl.ds(64 * h + start, count), :]
+                y = flat[block, pl.ds(64 * h + 32 + start, count), :]
+                c = leaf_cos[pl.ds(8 * h + child, 1), at]
+                s = leaf_sin[pl.ds(8 * h + child, 1), at]
+                pair.append((x * c - y * s, x * s + y * c))
             for component in range(2):
-                highs.append(jnp.concatenate([pair[0][component][0], pair[1][component][0]], axis=1))
-                lows.append(jnp.concatenate([pair[0][component][1], pair[1][component][1]], axis=1))
+                rows.append(jnp.concatenate([pair[0][component], pair[1][component]], axis=1))
+        high, low = halves(jnp.concatenate(rows, axis=0))
         w = low_weight[block]
-        y = product(jnp.concatenate(highs, axis=0), w) + product(jnp.concatenate(lows, axis=0), w)
-        parts[block] = y[:, :128] + y[:, 128:]
-
-    wide = iota((512, 128), 1)
+        y = product(high, w) + product(low, w)
+        return y[:, :128] + y[:, 128:]
+
+    wide = iota((16 * COUNT, 128), 1)
+
+    def copy(c, t, start):
+        here = (c, pl.ds(start, CHUNK), slice(None), pl.ds(128 * t, 128))
+        return pltpu.make_async_copy(result.at[here], out.at[here], sems.at[c, t, start // CHUNK])
+
+    def emit(start, t):
+        def step(i, carry):
+            for child in range(8):
+                to = pl.ds(8 * child, 8), pl.ds(128 * t, 128)
+                c, s = low_cos[to], low_sin[to]
+                for k in range(PER):
+                    r = PER * i + k
+                    x = low[pl.ds(2 * COUNT * child + r, 1), :]
+                    y = low[pl.ds(2 * COUNT * child + COUNT + r, 1), :]
+                    result[(0, start + r) + to] = x * c - y * s
+                    result[(1, start + r) + to] = x * s + y * c
+            for k in range(PER // CHUNK):
+                for c in range(2):
+                    copy(c, t, start + PER * i + CHUNK * k).start()
+            return carry
+
+        for i in range(COUNT // PER):
+            step(i, 0)
+
+    for part in range(32 // COUNT):
+        start = COUNT * part
+        for t, blocks in enumerate(((7, 0, 1, 2), (3, 4), (5, 6), ())):
+            for block in blocks:
+                parts[block] = anterpolate(block, start, COUNT)
+            here, there, after_, before_ = (parts[k % 8] for k in (2 * t, 2 * t + 1, 2 * t + 2, 2 * t + 7))
+            low[...] = jnp.where(wide >= 126, after_, here) + jnp.where(wide < 2, before_, there)
+            emit(start, t)
+
     for t in range(4):
-        here, there = parts[2 * t], parts[2 * t + 1]
-        total = jnp.where(
-            wide < 2,
-            here + parts[(2 * t + 7) % 8],
-            jnp.where(wide >= 126, there + parts[(2 * t + 2) % 8], here + there),
-        )
-        low[:, pl.ds(128 * t, 128)] = total
-
-    def copies(r):
-        return [pltpu.make_async_copy(result.at[c, r], out.at[c, r], sems.at[c, r]) for c in range(2)]
-
-    def step(r, carry):
-        for child in range(8):
-            x = low[pl.ds(64 * child + r, 1), :]
-            y = low[pl.ds(64 * child + 32 + r, 1), :]
-            c = low_cos[pl.ds(8 * child, 8), :]
-            s = low_sin[pl.ds(8 * child, 8), :]
-            result[0, r, pl.ds(8 * child, 8), :] = x * c - y * s
-            result[1, r, pl.ds(8 * child, 8), :] = x * s + y * c
-        for copy in copies(r):
-            copy.start()
-        return carry
-
-    lax.fori_loop(0, 32, step, 0)
-
-    def finish(r, carry):
-        for copy in copies(r):
-            copy.wait()
-        return carry
-
-    lax.fori_loop(0, 32, finish, 0)
+        for k in range(32 // CHUNK):
+            for c in range(2):
+                copy(c, t, CHUNK * k).wait()
 
 
 RECEIVE_SCRATCH = [
-    pltpu.VMEM((512, 128), F32),
-    pltpu.VMEM((1024, 128), F32),
-    pltpu.VMEM((8, 512, 128), F32),
-    pltpu.VMEM((512, 512), F32),
+    pltpu.VMEM((8, 128, 128), F32),
+    pltpu.VMEM((8, 16 * COUNT, 128), F32),
+    pltpu.VMEM((16 * COUNT, 128), F32),
     pltpu.VMEM((2, 32, 64, 512), F32),
-    pltpu.SemaphoreType.DMA((2, 32)),
+    pltpu.SemaphoreType.DMA((2, 4, 32 // CHUNK)),
 ]
 
 

time: 34.7 us -> 33.4 us (0.963)
  Pallas kernels: 13.7 us -> 11.4 us
  waiting for transfers between devices: 10.4 us -> 11.4 us
    pallas_call x1, Pallas kernels: 5.67 us -> 4.54 us  [receive(): pl.pallas_call(receive_kernel, out_shape=jax.ShapeDtypeStruct((2, 32, 64,...]
    pallas_call x1, Pallas kernels: 3.33 us -> 2.33 us  [tables(): pl.pallas_call(table_kernel, out_shape=[jax.ShapeDtypeStruct((16, 1024),...]
    all_to_all x1, waiting for transfers between devices: 10.4 us -> 11.4 us  [body(): lax.all_to_all(message, 'ang', split_axis=0, concat_axis=0, tiled=True)]
  transfers between devices with their start and end apart: 1 -> 1, of which waited for: 1 -> 1; matrix products, arithmetic and copies ran while one was open for 0% -> 0% of each run, Pallas kernels for 10% -> 7%
where the time goes in v3:
time: 33.4 us; the launch traced here: 33.2 us
  Pallas kernels  11.4 us (34%)
  waiting for transfers between devices  11.4 us (34%)
  starting transfers between devices  10.3 us (31%)
    all_to_all x1, waiting for transfers between devices, body(): lax.all_to_all(message, 'ang', split_axis=0, concat_axis=0, tiled=True)  11.4 us
    all_to_all x1, starting transfers between devices, body(): lax.all_to_all(message, 'ang', split_axis=0, concat_axis=0, tiled=True)  10.3 us
    pallas_call x1, Pallas kernels, receive(): pl.pallas_call(receive_kernel, out_shape=jax.ShapeDtypeStruct((2, 32, 64,...  4.54 us
    pallas_call x1, Pallas kernels, send(): pl.pallas_call(send_kernel, out_shape=jax.ShapeDtypeStruct((ANG * ROWS, 1...  4.52 us
    pallas_call x1, Pallas kernels, tables(): pl.pallas_call(table_kernel, out_shape=[jax.ShapeDtypeStruct((16, 1024),...  2.33 us
  transfers between devices with their start and end apart: 1, of which 1 were waited for; matrix products, arithmetic and copies ran while one was open for 0% of the time, Pallas kernels for 7%

profile of v3, /device:TPU:1, one launch (start us, length us, event | category | flops | bytes accessed | tf_op | source)
XLA Modules:
  0.0 33.2 jit_solution(17043807009283732300)
XLA Ops:
  0.0 4.5 %send.1 = f32[1344,128]{1,0:T(8,128)} custom-call(f32[2,32,8,512]{3,2,1,0:T(8,128)} %incoming.1, bf16[2,32,64,128]{3,2,1,0:T(8,128)(2,1)} %own.1, f32[64,128]{1,0:T(8,128)} %all_phase.1, f32[4,512]{1,0:T(4,128)} %all_top.1, f32[4,8192]{1,0:T(4,128)} %weight_leaf.1, s32[4]{0:T(128)} %offsets.1, s32[4,64]{1,0:T(4,128)} %all_owner.1), custom_call_target="tpu_custom_call" | custom-call | tf_op jit(solution)/shard_map/send/pallas_call | solution.py:219
  4.5 10.3 %all-to-all-start = ((f32[64,1,2688]{2,1,0:T(1,128)}), f32[64,1,2688]{2,1,0:T(1,128)S(1)}, u32[]{:S(2)}, u32[]{:S(2)}) async-start(f32[64,1,2688]{2,1,0:T(1,128)} %bitcast), calls=%async_computation | async-start | bytes 1376256 | tf_op jit(solution)/shard_map/all_to_all | solution.py:461
  14.9 2.3 %tables.1 = (f32[16,1024]{1,0:T(8,128)S(1)}, f32[16,1024]{1,0:T(8,128)S(1)}, f32[64,512]{1,0:T(8,128)S(1)}, f32[64,512]{1,0:T(8,128)S(1)}, bf16[8,256,256]{2,1,0:T(8,128)(2,1)S(1)}, /*index=5*/f32[10,64,128]{2,1,0:T(8,128)S(1)}) custom-call(f32[8,2048]{1,0:T(8,128)} %phase_leaf.1, f32[64,512]{1,0:T(8,128)} %phase_low.1, f32[4,2048]{1,0:T(4,128)} %weight_low.1, ...), custom_call_target="tpu_custom_call" | custom-call | tf_op jit(solution)/shard_map/tables/pallas_call | solution.py:294
  17.2 11.4 %all-to-all-done = f32[64,1,2688]{2,1,0:T(1,128)S(1)} async-done(((f32[64,1,2688]{2,1,0:T(1,128)}), f32[64,1,2688]{2,1,0:T(1,128)S(1)}, u32[]{:S(2)}, u32[]{:S(2)}) %all-to-all-start) | async-done | bytes 688160 | tf_op jit(solution)/shard_map/all_to_all | solution.py:461
  28.6 4.5 %receive.1 = f32[2,32,64,512]{3,2,1,0:T(8,128)} custom-call(f32[1344,128]{1,0:T(8,128)S(1)} %bitcast.2, f32[16,1024]{1,0:T(8,128)S(1)} %get-tuple-element.11.leaf_cos, f32[16,1024]{1,0:T(8,128)S(1)} %get-tuple-element.12.leaf_sin, f32[64,512]{1,0:T(8,128)S(1)} %get-tuple-element.13.low_cos, f32[64,512]{1,0:T(8,128)S(1)} %get-tuple-element.14.low_sin, ...), custom_call_target="tpu_custom_call" | custom-call | tf_op jit(solution)/shard_map/receive/pallas_call | solution.py:437
Async XLA Ops:
  4.5 24.1 %all-to-all-start = ((f32[64,1,2688]{2,1,0:T(1,128)}), f32[64,1,2688]{2,1,0:T(1,128)S(1)}, u32[]{:S(2)}, u32[]{:S(2)}) async-start(f32[64,1,2688]{2,1,0:T(1,128)} %bitcast), calls=%async_computation | async-start | bytes 1376256 | tf_op jit(solution)/shard_map/all_to_all | solution.py:461

commit v4 on v3

--- a/solution.py
+++ b/solution.py
@@ -14,6 +14,13 @@
 COUNT = 16
 PER = 16
 CHUNK = 16
+ORDER = (
+    53, 29, 32, 22, 39, 40, 28, 26, 50, 42, 49, 20, 55, 43, 58, 47,
+    0, 57, 37, 2, 8, 15, 24, 31, 7, 38, 36, 21, 52, 60, 27, 56,
+    45, 51, 62, 10, 12, 44, 41, 54, 13, 16, 61, 11, 17, 23, 34, 33,
+    14, 3, 48, 18, 35, 59, 1, 4, 5, 9, 63, 25, 46, 6, 19, 30,
+)
+PLACE = tuple(ORDER.index(g) for g in range(ANG))
 NT = (((1,), (1,)), ((), ()))
 F32 = jnp.float32
 BF16 = jnp.bfloat16
@@ -73,7 +80,7 @@
 
 def send_kernel(
     incoming, own, all_phase, all_top, all_leaf, all_offsets, all_owner, message,
-    fine, field, phase, weight_top, local, offsets, owner, spread_own, coarse, rims, sems,
+    fine, field, phase, weight_top, local, offsets, owner, place, spread_own, coarse, rims, sems,
 ):
     ang = lax.axis_index("ang")
     box = lax.axis_index("box")
@@ -97,6 +104,8 @@
     for copy in small + get_fine + get_field:
         copy.start()
 
+    for g in range(ANG):
+        place[g] = PLACE[g]
     small[0].wait()
     cosine, sine = turn(phase[...])
     lane = iota((64, 128), 1)
@@ -209,7 +218,7 @@
                         tile = jnp.where(half, pltpu.roll(a, 64, 1), d)
                     else:
                         tile = jnp.where(half, a, pltpu.roll(d, 64, 1))
-                    target = owner[box, b] * ROWS
+                    target = place[owner[box, b]] * ROWS
                     extra = rim_tiles[p] + jnp.where(fifth, rim_phase[b : b + 1], 0.0)
                     message[pl.ds(target, 16), :] = tile[:16]
                     message[pl.ds(target + 16, 5), :] = (tile[16:] + extra)[:5]
@@ -235,6 +244,7 @@
     pltpu.VMEM((4, 128), F32),
     pltpu.SMEM((4,), jnp.int32),
     pltpu.SMEM((4, 64), jnp.int32),
+    pltpu.SMEM((64,), jnp.int32),
     pltpu.VMEM((64 * PITCH, 128), F32),
     pltpu.VMEM((512, 128), F32),
     pltpu.VMEM((512, 128), F32),
@@ -316,8 +326,11 @@
     side = iota((64, 128), 1) < 64
     lane = iota((64, 128), 1)
 
+    def rows_of(sources, i):
+        return jnp.concatenate([got[pl.ds(ROWS * PLACE[g] + i, 1), :] for g in sources], axis=0)
+
     def line(i):
-        return got[pl.ds(16 + i, 64, stride=ROWS), :]
+        return rows_of(range(ANG), 16 + i)
 
     cs = line(4)
 
@@ -360,7 +373,7 @@
     for block in range(8):
         tiles = []
         for i in range(16):
-            tile = got[pl.ds(8 * ROWS * block + i, 8, stride=ROWS), :]
+            tile = rows_of(range(8 * block, 8 * block + 8), i)
             if i in rows:
                 tile = tile + rows[i][8 * block : 8 * block + 8]
             tiles.append(tile)
@@ -458,7 +471,7 @@
     )
     message = send(incoming, own_field, phase_mid, weight_top, weight_leaf, offsets, owner)
     message = message.reshape(ANG, 1, ROWS * 128)
-    got = lax.all_to_all(message, "ang", split_axis=0, concat_axis=0, tiled=True)
+    got = lax.all_to_all(message, "ang", split_axis=0, concat_axis=0, tiled=True, axis_index_groups=[list(ORDER)])
     got = got.reshape(ANG * ROWS, 128)
     ready = tables(phase_leaf, phase_low, weight_low, weight_leaf, offsets)
     return receive(got, ready)

time: 33.4 us -> 29.7 us (0.89)
  waiting for transfers between devices: 11.4 us -> 5.92 us
  starting transfers between devices: 10.3 us -> 12 us
    all_to_all x1, waiting for transfers between devices: 11.4 us -> 5.92 us  [body(): lax.all_to_all(message, 'ang', split_axis=0, concat_axis=0, tiled=True, a...]
    all_to_all x1, starting transfers between devices: 10.3 us -> 12 us  [body(): lax.all_to_all(message, 'ang', split_axis=0, concat_axis=0, tiled=True, a...]
  transfers between devices with their start and end apart: 1 -> 1, of which waited for: 1 -> 1; matrix products, arithmetic and copies ran while one was open for 0% -> 0% of each run, Pallas kernels for 7% -> 8%
where the time goes in v4:
time: 29.7 us; the launch traced here: 29.5 us
  starting transfers between devices  12 us (40%)
  Pallas kernels  11.6 us (39%)
  waiting for transfers between devices  5.92 us (20%)
    all_to_all x1, starting transfers between devices, body(): lax.all_to_all(message, 'ang', split_axis=0, concat_axis=0, tiled=True, a...  12 us
    all_to_all x1, waiting for transfers between devices, body(): lax.all_to_all(message, 'ang', split_axis=0, concat_axis=0, tiled=True, a...  5.92 us
    pallas_call x1, Pallas kernels, receive(): pl.pallas_call(receive_kernel, out_shape=jax.ShapeDtypeStruct((2, 32, 64,...  4.72 us
    pallas_call x1, Pallas kernels, send(): pl.pallas_call(send_kernel, out_shape=jax.ShapeDtypeStruct((ANG * ROWS, 1...  4.52 us
    pallas_call x1, Pallas kernels, tables(): pl.pallas_call(table_kernel, out_shape=[jax.ShapeDtypeStruct((16, 1024),...  2.33 us
  transfers between devices with their start and end apart: 1, of which 1 were waited for; matrix products, arithmetic and copies ran while one was open for 0% of the time, Pallas kernels for 8%

profile of v4, /device:TPU:1, one launch (start us, length us, event | category | flops | bytes accessed | tf_op | source)
XLA Modules:
  0.0 29.5 jit_solution(13057953253721500988)
XLA Ops:
  0.0 4.5 %send.1 = f32[1344,128]{1,0:T(8,128)} custom-call(f32[2,32,8,512]{3,2,1,0:T(8,128)} %incoming.1, bf16[2,32,64,128]{3,2,1,0:T(8,128)(2,1)} %own.1, f32[64,128]{1,0:T(8,128)} %all_phase.1, f32[4,512]{1,0:T(4,128)} %all_top.1, f32[4,8192]{1,0:T(4,128)} %weight_leaf.1, s32[4]{0:T(128)} %offsets.1, s32[4,64]{1,0:T(4,128)} %all_owner.1), custom_call_target="tpu_custom_call" | custom-call | tf_op jit(solution)/shard_map/send/pallas_call | solution.py:228
  4.5 12.0 %all-to-all-start = ((f32[64,1,2688]{2,1,0:T(1,128)}), f32[64,1,2688]{2,1,0:T(1,128)S(1)}, u32[]{:S(2)}, u32[]{:S(2)}) async-start(f32[64,1,2688]{2,1,0:T(1,128)} %bitcast), calls=%async_computation | async-start | bytes 1376256 | tf_op jit(solution)/shard_map/all_to_all | solution.py:474
  16.5 2.3 %tables.1 = (f32[16,1024]{1,0:T(8,128)S(1)}, f32[16,1024]{1,0:T(8,128)S(1)}, f32[64,512]{1,0:T(8,128)S(1)}, f32[64,512]{1,0:T(8,128)S(1)}, bf16[8,256,256]{2,1,0:T(8,128)(2,1)S(1)}, /*index=5*/f32[10,64,128]{2,1,0:T(8,128)S(1)}) custom-call(f32[8,2048]{1,0:T(8,128)} %phase_leaf.1, f32[64,512]{1,0:T(8,128)} %phase_low.1, f32[4,2048]{1,0:T(4,128)} %weight_low.1, ...), custom_call_target="tpu_custom_call" | custom-call | tf_op jit(solution)/shard_map/tables/pallas_call | solution.py:304
  18.9 5.9 %all-to-all-done = f32[64,1,2688]{2,1,0:T(1,128)S(1)} async-done(((f32[64,1,2688]{2,1,0:T(1,128)}), f32[64,1,2688]{2,1,0:T(1,128)S(1)}, u32[]{:S(2)}, u32[]{:S(2)}) %all-to-all-start) | async-done | bytes 688160 | tf_op jit(solution)/shard_map/all_to_all | solution.py:474
  24.8 4.7 %receive.1 = f32[2,32,64,512]{3,2,1,0:T(8,128)} custom-call(f32[1344,128]{1,0:T(8,128)S(1)} %bitcast.2, f32[16,1024]{1,0:T(8,128)S(1)} %get-tuple-element.11.leaf_cos, f32[16,1024]{1,0:T(8,128)S(1)} %get-tuple-element.12.leaf_sin, f32[64,512]{1,0:T(8,128)S(1)} %get-tuple-element.13.low_cos, f32[64,512]{1,0:T(8,128)S(1)} %get-tuple-element.14.low_sin, ...), custom_call_target="tpu_custom_call" | custom-call | tf_op jit(solution)/shard_map/receive/pallas_call | solution.py:450
Async XLA Ops:
  4.5 20.3 %all-to-all-start = ((f32[64,1,2688]{2,1,0:T(1,128)}), f32[64,1,2688]{2,1,0:T(1,128)S(1)}, u32[]{:S(2)}, u32[]{:S(2)}) async-start(f32[64,1,2688]{2,1,0:T(1,128)} %bitcast), calls=%async_computation | async-start | bytes 1376256 | tf_op jit(solution)/shard_map/all_to_all | solution.py:474
